TPU v7x, 32 devices: a whole 2x2x4 slice. The times are simulated.
32 devices in a mesh: ctx: 32 (over z, y, x, core), head: 1.
Axes of the slice: x: 2, y: 2, z: 4, core: 2. Of those that a mesh axis runs over, the one named last changes fastest.
Arguments:
- queries: bfloat16 [6144, 4096], P('ctx', 'head'), may hold values from -6 to 6
- keys: bfloat16 [6144, 1024], P('ctx', 'head'), may hold values from -6 to 6
- values: bfloat16 [6144, 1024], P('ctx', 'head'), may hold values from -6 to 6
- retrieval: int32 [32], replicated, may hold values 0 or 1
- spans: int32 [2, 32], replicated, may hold values from 64 to 4096, as said below
- out_weight: bfloat16 [4096, 4096], P(None, 'head'), may hold values from -0.09375 to 0.09375
Outputs:
- layer_out: bfloat16 [6144, 4096], P('ctx', 'head')
Inputs may be any that keep to these rules, and one draw needn't show every extreme that they name: `spans`: row 0 lies within 64 to 128, row 1 within 2048 to 4096; some head has exactly 128 sink tokens and some head exactly 4096 recent tokens.
All inputs are finite; a program needn't handle non-finite values.
Results may differ from a plain program's by a relative error of at most 0.0075.
Values may be sent and summed in bfloat16 or wider, within the bound.
A program may use at most 192 MiB of HBM per device.

v0:
```python
import jax
import jax.numpy as jnp
from jax import lax
from jax.sharding import PartitionSpec as P

HD = 128


def body(queries, keys, values, retrieval, spans, out_weight):
    row_count = queries.shape[0]
    half_rows = row_count // 2
    local_heads = queries.shape[1] // HD
    kv_heads = keys.shape[1] // HD
    group_size = local_heads // kv_heads
    scale = HD ** (-0.5)
    head_first = lax.axis_index("head") * local_heads
    retrieval_heads = (
        lax.dynamic_slice_in_dim(retrieval, head_first, local_heads).reshape(kv_heads, group_size)
        > 0
    )
    sink_sizes = lax.dynamic_slice_in_dim(spans[0], head_first, local_heads).reshape(
        kv_heads, group_size
    )
    window_sizes = lax.dynamic_slice_in_dim(spans[1], head_first, local_heads).reshape(
        kv_heads, group_size
    )
    cycle_index = lax.axis_index("ctx")
    near_queries = queries[:half_rows]
    far_queries = queries[half_rows:]
    near_pos = cycle_index * row_count + jnp.arange(half_rows, dtype=jnp.int32)
    far_pos = cycle_index * row_count + half_rows + jnp.arange(half_rows, dtype=jnp.int32)
    near_heads = near_queries.reshape(half_rows, kv_heads, group_size, HD)
    far_heads = far_queries.reshape(half_rows, kv_heads, group_size, HD)

    def update(state, query_heads, query_pos, key_heads, value_heads, key_pos):
        maxima, totals, accum = state
        scores = (
            jnp.einsum("qgjd,kgd->qgjk", query_heads, key_heads, preferred_element_type=jnp.float32)
            * scale
        )
        gap = query_pos[:, None] - key_pos[None, :]
        reach = retrieval_heads[None, :, :, None] | (
            key_pos[None, None, None, :] < sink_sizes[None, :, :, None]
        )
        reach = reach | (gap[:, None, None, :] < window_sizes[None, :, :, None])
        allowed = (gap >= 0)[:, None, None, :] & reach
        masked = jnp.where(allowed, scores, -1e30)
        fresh = jnp.maximum(maxima, jnp.max(masked, axis=-1))
        weights = jnp.where(allowed, jnp.exp(masked - fresh[..., None]), 0.0)
        totals = jnp.sum(weights, axis=-1)
        added = jnp.einsum(
            "qgjk,kgd->qgjd",
            weights.astype(jnp.bfloat16),
            value_heads,
            preferred_element_type=jnp.float32,
        )
        accum = added
        return (fresh, totals, accum)

    def visit(state, query_heads, query_pos, key_heads, value_heads, key_pos, offset):

        def active(held):
            return update(held, query_heads, query_pos, key_heads, value_heads, key_pos)

        def skipped(held):
            return held

        return lax.cond(offset <= query_pos[-1], active, skipped, state)

    start_state = (
        jnp.full((half_rows, kv_heads, group_size), -1e30, jnp.float32),
        jnp.zeros((half_rows, kv_heads, group_size), jnp.float32),
        jnp.zeros((half_rows, kv_heads, group_size, HD), jnp.float32),
    )
    pieces = (
        lax.all_gather(keys, "ctx", axis=0, tiled=True),
        lax.all_gather(values, "ctx", axis=0, tiled=True),
    )
    offset = jnp.int32(0)
    key_rows = pieces[0].shape[0]
    key_heads = pieces[0].reshape(key_rows, kv_heads, HD)
    value_heads = pieces[1].reshape(key_rows, kv_heads, HD)
    key_pos = jnp.arange(key_rows, dtype=jnp.int32)
    near_state = visit(start_state, near_heads, near_pos, key_heads, value_heads, key_pos, offset)
    far_state = visit(start_state, far_heads, far_pos, key_heads, value_heads, key_pos, offset)
    near_state, far_state = (near_state, far_state)

    def finish(state):
        return (
            (state[2] / state[1][..., None])
            .reshape(half_rows, local_heads * HD)
            .astype(jnp.bfloat16)
        )

    near_attended = finish(near_state)
    far_attended = finish(far_state)
    attended = jnp.concatenate([near_attended, far_attended], axis=0)
    features = lax.all_gather(attended, "head", axis=1, tiled=True)
    projected = jnp.dot(features, out_weight, preferred_element_type=jnp.float32)
    return projected.astype(jnp.bfloat16)


def solution(mesh):
    in_specs = (P("ctx", "head"), P("ctx", "head"), P("ctx", "head"), P(), P(), P(None, "head"))
    out_specs = P("ctx", "head")
    return jax.shard_map(body, mesh=mesh, in_specs=in_specs, out_specs=out_specs, check_vma=False)
```

profile of v0, /device:TPU:0, one launch (start us, length us, event | category | flops | bytes accessed | tf_op | source)
XLA Modules:
  0.0 474.7 jit_solution(1809647474993605472)
XLA Ops:
  6.5 0.7 all-gather.3.cloned.1.call-update
  7.3 0.7 all-gather.5.cloned.1.call-update
  8.0 0.6 slice.20
  9.3 0.6 slice.23
  10.5 0.7 broadcast_compare_fusion.2
  11.3 0.8 slice_bitcast_fusion
  12.0 96.1 %all-gather.3.cloned.1.call-done = bf16[6144,1024]{1,0:T(8,128)(2,1)} async-done(((bf16[192,1024]{1,0:T(8,128)(2,1)}), bf16[6144,1024]{1,0:T(8,128)(2,1)}) %all-gather.3.cloned.1.call-update) | async-done | bytes 12582928 | tf_op jit(solution)/shard_map/all_gather | solution.py:76
  108.1 16.8 %copy.23 = bf16[6144,1024]{0,1:T(8,128)(2,1)} copy(bf16[6144,1024]{1,0:T(8,128)(2,1)} %all-gather.3.cloned.1.call-done) | data formatting | bytes 25165824 | tf_op jit(solution)/shard_map/all_gather | solution.py:76
  124.9 79.9 %all-gather.5.cloned.1.call-done = bf16[6144,1024]{1,0:T(8,128)(2,1)} async-done(((bf16[192,1024]{1,0:T(8,128)(2,1)}), bf16[6144,1024]{1,0:T(8,128)(2,1)}) %all-gather.5.cloned.1.call-update) | async-done | bytes 12582928 | tf_op jit(solution)/shard_map/all_gather | solution.py:77
  204.8 16.7 %copy.24 = bf16[6144,1024]{0,1:T(8,128)(2,1)} copy(bf16[6144,1024]{1,0:T(8,128)(2,1)} %all-gather.5.cloned.1.call-done) | data formatting | bytes 25165824 | tf_op jit(solution)/shard_map/all_gather | solution.py:77
  221.5 111.5 %conditional.2 = (f32[96,8,4]{0,2,1:T(4,128)S(1)}, f32[96,8,4,128]{3,0,2,1:T(8,128)}) conditional(s32[]{:T(128)} %bitcast.8, () %tuple.21, (s32[96]{0:T(128)S(1)}, s32[6144]{0:T(1024)S(1)}, pred[8,4]{1,0:T(8,128)(4,1)S(1)}, s32[6144]{0:T(1024)S(1)}, s32[32]{0:T(128)S(1)}, /*index=5*/s32[32]{0:T(128)S(1)}, bf16[192,4096]{1,0:T(8,128)(2,1)S(1)}, ...), branch_computations={%region_0.0_spmd, %region_1.4_spmd} | conditional | flops 10081072128 | bytes 269895488 | solution.py:68
  221.7 0.3 compare_or_fusion
  222.0 0.4 broadcast_compare_fusion
  222.5 1.4 reshape.145
  224.2 34.7 %fusion = (f32[96,8,4]{0,2,1:T(4,128)S(1)}, f32[8,6144,96,4]{1,2,3,0:T(8,128)}) fusion(s32[8,4]{1,0:T(8,128)S(1)} %lt.62, s32[96,6144]{1,0:T(8,128)S(1)} %broadcast_subtract_fusion, pred[8,4,6144]{2,1,0:T(4,128)(4,1)S(1)} %compare_or_fusion, pred[96,6144]{1,0:T(8,128)(4,1)S(1)} %broadcast_compare_fusion, bf16[96,8,4,128]{3,2,1,0:T(4,128)(2,1)} %reshape.145, ...), kind=kOutput, calls=%fused_computation.3 | convolution fusion | flops 4945081344 | bytes 92024960 | tf_op jit(solution)/shard_map/cond/branch_1_fun/qgjd,kgd->qgjk/dot_general | solution.py:38
  259.0 35.2 %fusion.10 = f32[96,8,4,128]{3,0,2,1:T(8,128)} fusion(bf16[6144,8,128]{0,2,1:T(8,128)(2,1)} %get-tuple-element.95, f32[8,6144,96,4]{1,2,3,0:T(8,128)} %get-tuple-element.106, f32[96,8,4]{0,2,1:T(4,128)S(1)} %broadcast_maximum_fusion, s32[8,4]{1,0:T(8,128)S(1)} %lt.62, s32[96,6144]{1,0:T(8,128)S(1)} %broadcast_subtract_fusion, ...), kind=kOutput, calls=%fused_computation.12 | convolution fusion | flops 4982833152 | bytes 92811392 | tf_op jit(solution)/shard_map/cond/branch_1_fun/qgjk,kgd->qgjd/dot_general | solution.py:51
  294.2 38.6 %fusion.2 = f32[96,8,4]{0,2,1:T(4,128)S(1)} fusion(f32[8,6144,96,4]{1,2,3,0:T(8,128)} %get-tuple-element.106, f32[96,8,4]{0,2,1:T(4,128)S(1)} %broadcast_maximum_fusion, s32[8,4]{1,0:T(8,128)S(1)} %lt.62, s32[96,6144]{1,0:T(8,128)S(1)} %broadcast_subtract_fusion, pred[8,4,6144]{2,1,0:T(4,128)(4,1)S(1)} %compare_or_fusion, ...), kind=kLoop, calls=%fused_computation.5 | loop fusion | flops 150991872 | bytes 78667904 | tf_op jit(solution)/shard_map/cond/branch_1_fun/reduce_sum | solution.py:50
  333.0 1.9 divide_convert_fusion.1
  334.9 0.4 copy.27
  335.3 1.5 convert_element_type.36
  336.8 112.8 %conditional.3 = (f32[96,8,4]{0,2,1:T(4,128)S(1)}, f32[96,8,4,128]{3,0,2,1:T(8,128)}) conditional(s32[]{:T(128)} %bitcast.13, () %tuple.23, (s32[96]{0:T(128)S(1)}, s32[6144]{0:T(1024)S(1)}, pred[8,4]{1,0:T(8,128)(4,1)S(1)}, s32[6144]{0:T(1024)S(1)}, s32[32]{0:T(128)S(1)}, /*index=5*/s32[32]{0:T(128)S(1)}, bf16[192,4096]{1,0:T(8,128)(2,1)}, ...), branch_computations={%region_4.5_spmd, %region_5.8_spmd} | conditional | flops 10081072128 | bytes 269895488 | solution.py:68
  336.9 0.3 compare_or_fusion.1
  337.3 0.4 broadcast_compare_fusion.1
  337.7 1.2 slice.15
  338.9 1.4 reshape.146
  340.6 34.8 %fusion.19 = (f32[96,8,4]{0,2,1:T(4,128)S(1)}, f32[8,6144,96,4]{1,2,3,0:T(8,128)}) fusion(s32[8,4]{1,0:T(8,128)S(1)} %lt.70, s32[96,6144]{1,0:T(8,128)S(1)} %broadcast_subtract_fusion.1, pred[8,4,6144]{2,1,0:T(4,128)(4,1)S(1)} %compare_or_fusion.1, pred[96,6144]{1,0:T(8,128)(4,1)S(1)} %broadcast_compare_fusion.1, bf16[96,8,4,128]{3,2,1,0:T(4,128)(2,1)} %reshape.146, ...), kind=kOutput, calls=%fused_computation.24 | convolution fusion | flops 4945081344 | bytes 92024960 | tf_op jit(solution)/shard_map/cond/branch_1_fun/qgjd,kgd->qgjk/dot_general | solution.py:38
  375.4 35.2 %fusion.29 = f32[96,8,4,128]{3,0,2,1:T(8,128)} fusion(bf16[6144,8,128]{0,2,1:T(8,128)(2,1)} %get-tuple-element.104, f32[8,6144,96,4]{1,2,3,0:T(8,128)} %get-tuple-element.108, f32[96,8,4]{0,2,1:T(4,128)S(1)} %broadcast_maximum_fusion.1, s32[8,4]{1,0:T(8,128)S(1)} %lt.70, s32[96,6144]{1,0:T(8,128)S(1)} %broadcast_subtract_fusion.1, ...), kind=kOutput, calls=%fused_computation.33 | convolution fusion | flops 4982833152 | bytes 92811392 | tf_op jit(solution)/shard_map/cond/branch_1_fun/qgjk,kgd->qgjd/dot_general | solution.py:51
  410.7 38.6 %fusion.21 = f32[96,8,4]{0,2,1:T(4,128)S(1)} fusion(f32[8,6144,96,4]{1,2,3,0:T(8,128)} %get-tuple-element.108, f32[96,8,4]{0,2,1:T(4,128)S(1)} %broadcast_maximum_fusion.1, s32[8,4]{1,0:T(8,128)S(1)} %lt.70, s32[96,6144]{1,0:T(8,128)S(1)} %broadcast_subtract_fusion.1, pred[8,4,6144]{2,1,0:T(4,128)(4,1)S(1)} %compare_or_fusion.1, ...), kind=kLoop, calls=%fused_computation.26 | loop fusion | flops 150991872 | bytes 78667904 | tf_op jit(solution)/shard_map/cond/branch_1_fun/reduce_sum | solution.py:50
  449.5 1.9 divide_convert_fusion
  451.4 0.4 copy.30
  451.9 0.6 convert_element_type.40
  452.5 15.4 %convolution_convert_fusion = bf16[192,4096]{1,0:T(8,128)(2,1)} fusion(bf16[4096,4096]{1,0:T(8,128)(2,1)} %param.15, bf16[96,4096]{1,0:T(8,128)(2,1)S(1)} %convert_element_type.40, bf16[96,4096]{1,0:T(8,128)(2,1)} %convert_element_type.36), kind=kOutput, calls=%fused_computation.42 | convolution fusion | flops 6446383104 | bytes 36700160 | tf_op jit(solution)/shard_map/dot_general | solution.py:99
  (22 shorter events, 1.0 us)
Async XLA Ops:
  6.5 101.6 %all-gather.3.cloned.1.call-start = ((), (), s32[]{:S(2)}) async-start(), calls=%async_computation | async-start | bytes 12976128 | tf_op jit(solution)/shard_map/all_gather | solution.py:76
  7.3 197.5 %all-gather.5.cloned.1.call-start = ((), (), s32[]{:S(2)}) async-start(), calls=%async_computation.1 | async-start | bytes 12976128 | tf_op jit(solution)/shard_map/all_gather | solution.py:77
  9.3 1.2 copy-start.1
  124.9 96.6 %copy-start = (bf16[192,4096]{1,0:T(8,128)(2,1)S(1)}, bf16[192,4096]{1,0:T(8,128)(2,1)}, u32[]{:S(2)}) copy-start(bf16[192,4096]{1,0:T(8,128)(2,1)} %param.10) | copy-start | bytes 4718596
  221.5 115.3 %copy-start.2 = (s32[96]{0:T(128)S(1)}, s32[96]{0:T(128)}, u32[]{:S(2)}) copy-start(s32[96]{0:T(128)} %copy-done.1) | copy-start | bytes 1156
Sparse Core Ops, SparseCore 0:
  10.2 97.8 all-gather.2
  111.0 93.7 all-gather.4
where the time goes:
time: 476 us; the launch traced here: 475 us
  waiting for transfers between devices  177 us (37%)
  matrix products  155 us (33%)
  other arithmetic  83.7 us (18%)
  local copies, waits for them, and re-layouts  42.8 us (9%)
  between operations  14.8 us (3%)
    all_gather x1, waiting for transfers between devices, body(): lax.all_gather(keys, 'ctx', axis=0, tiled=True)  96.1 us
    all_gather x1, waiting for transfers between devices, body(): lax.all_gather(values, 'ctx', axis=0, tiled=True)  79.9 us
    reduce_sum x2, other arithmetic, update(): totals = jnp.sum(weights, axis=-1)  77.2 us
    dot_general x2, matrix products, update(): jnp.einsum('qgjk,kgd->qgjd', weights.astype(jnp.bfloat16), value_heads, p...  70.4 us
    dot_general x2, matrix products, update(): jnp.einsum('qgjd,kgd->qgjk', query_heads, key_heads, preferred_element_ty...  69.5 us
    all_gather x1, local copies, waits for them, and re-layouts, body(): lax.all_gather(keys, 'ctx', axis=0, tiled=True)  16.8 us
    all_gather x1, local copies, waits for them, and re-layouts, body(): lax.all_gather(values, 'ctx', axis=0, tiled=True)  16.7 us
    dot_general x1, matrix products, body(): jnp.dot(features, out_weight, preferred_element_type=jnp.float32)  15.4 us
  transfers between devices with their start and end apart: 2, of which 2 were waited for; matrix products, arithmetic and copies ran while one was open for 4% of the time, Pallas kernels for 0%

commit v1 on v0

--- a/solution.py
+++ b/solution.py
@@ -2,6 +2,7 @@
 import jax.numpy as jnp
 from jax import lax
 from jax.sharding import PartitionSpec as P
+from jax.lax import all_to_all, axis_size
 
 HD = 128
 
@@ -72,10 +73,11 @@
         jnp.zeros((half_rows, kv_heads, group_size), jnp.float32),
         jnp.zeros((half_rows, kv_heads, group_size, HD), jnp.float32),
     )
-    pieces = (
-        lax.all_gather(keys, "ctx", axis=0, tiled=True),
-        lax.all_gather(values, "ctx", axis=0, tiled=True),
+    bands_scan = lambda target, group_axis: jnp.concatenate(
+        all_to_all(jnp.stack([target for _ in range(axis_size(group_axis))]), group_axis, 0, 0),
+        axis=0,
     )
+    pieces = (bands_scan(keys, "ctx"), lax.all_gather(values, "ctx", axis=0, tiled=True))
     offset = jnp.int32(0)
     key_rows = pieces[0].shape[0]
     key_heads = pieces[0].reshape(key_rows, kv_heads, HD)

time: 476 us -> 649 us (1.36)
  waiting for transfers between devices: 177 us -> 333 us
  starting transfers between devices: 0.04 us -> 7.48 us
    all_to_all x0 -> x1, waiting for transfers between devices: none -> 332 us  [body(): all_to_all(jnp.stack([target for _ in range(axis_size(group_axis))]), gro...]
    all_gather x1 -> x0, waiting for transfers between devices: 96.1 us -> none  [body(): lax.all_gather(keys, 'ctx', axis=0, tiled=True)]
    all_gather x1, waiting for transfers between devices: 79.9 us -> 0.01 us  [body(): lax.all_gather(values, 'ctx', axis=0, tiled=True)]
    all_gather x1 -> x0, local copies, waits for them, and re-layouts: 16.8 us -> none  [body(): lax.all_gather(keys, 'ctx', axis=0, tiled=True)]
    unnamed x6 -> x7, local copies, waits for them, and re-layouts: 0.01 us -> 11.9 us
    all_to_all x0 -> x1, starting transfers between devices: none -> 7.44 us  [body(): all_to_all(jnp.stack([target for _ in range(axis_size(group_axis))]), gro...]
    another operation x0 -> x1, local copies, waits for them, and re-layouts: none -> 7.21 us  [body(): jnp.stack([target for _ in range(axis_size(group_axis))])]
  transfers between devices with their start and end apart: 2 -> 2, of which waited for: 2 -> 1; matrix products, arithmetic and copies ran while one was open for 4% -> 2% of each run, Pallas kernels for 0% -> 0%
where the time goes in v1:
time: 649 us; the launch traced here: 644 us
  waiting for transfers between devices  333 us (51%)
  matrix products  161 us (25%)
  other arithmetic  83 us (13%)
  local copies, waits for them, and re-layouts  44.5 us (7%)
  between operations  15 us (2%)
  starting transfers between devices  7.48 us (1%)
    all_to_all x1, waiting for transfers between devices, body(): all_to_all(jnp.stack([target for _ in range(axis_size(group_axis))]), gro...  332 us
    reduce_sum x2, other arithmetic, update(): totals = jnp.sum(weights, axis=-1)  77.2 us
    dot_general x2, matrix products, update(): jnp.einsum('qgjd,kgd->qgjk', query_heads, key_heads, preferred_element_ty...  75.1 us
    dot_general x2, matrix products, update(): jnp.einsum('qgjk,kgd->qgjd', weights.astype(jnp.bfloat16), value_heads, p...  70.6 us
    all_gather x1, local copies, waits for them, and re-layouts, body(): lax.all_gather(values, 'ctx', axis=0, tiled=True)  16.8 us
    dot_general x1, matrix products, body(): jnp.dot(features, out_weight, preferred_element_type=jnp.float32)  15.4 us
  transfers between devices with their start and end apart: 2, of which 1 were waited for; matrix products, arithmetic and copies ran while one was open for 2% of the time, Pallas kernels for 0%

profile of v1, /device:TPU:0, one launch (start us, length us, event | category | flops | bytes accessed | tf_op | source)
XLA Modules:
  0.0 644.5 jit_solution(3252595035577842336)
XLA Ops:
  6.5 7.2 %stack.2 = bf16[32,192,1024]{2,1,0:T(8,128)(2,1)} broadcast(bf16[192,1024]{1,0:T(8,128)(2,1)} %param.11), dimensions={1,2} | broadcast | bytes 12976128 | tf_op jit(solution)/shard_map/stack | solution.py:77
  13.8 7.4 %all-to-all-start = ((bf16[32,192,1024]{2,1,0:T(8,128)(2,1)}), bf16[32,192,1024]{2,1,0:T(8,128)(2,1)}, u32[]{:S(2)}, u32[]{:S(2)}) async-start(bf16[32,192,1024]{2,1,0:T(8,128)(2,1)} %stack.2), calls=%async_computation | async-start | bytes 25165824 | tf_op jit(solution)/shard_map/all_to_all | solution.py:77
  21.2 0.7 all-gather.2.cloned.1.call-update
  22.0 0.6 slice.20
  23.2 0.6 slice.23
  24.6 331.9 %all-to-all-done = bf16[32,192,1024]{2,1,0:T(8,128)(2,1)} async-done(((bf16[32,192,1024]{2,1,0:T(8,128)(2,1)}), bf16[32,192,1024]{2,1,0:T(8,128)(2,1)}, u32[]{:S(2)}, u32[]{:S(2)}) %all-to-all-start) | async-done | bytes 12582944 | tf_op jit(solution)/shard_map/all_to_all | solution.py:77
  356.4 11.9 %copy.41 = bf16[768,8,8,128]{3,2,1,0:T(8,128)(2,1)} copy(bf16[768,8,8,128]{3,1,2,0:T(8,128)(2,1)} %bitcast.18) | data formatting | bytes 25165824
  368.3 16.8 %copy.22 = bf16[6144,1024]{0,1:T(8,128)(2,1)} copy(bf16[6144,1024]{1,0:T(8,128)(2,1)} %all-gather.2.cloned.1.call-done) | data formatting | bytes 25165824 | tf_op jit(solution)/shard_map/all_gather | solution.py:80
  385.1 114.0 %conditional.2 = (f32[96,8,4]{0,2,1:T(4,128)S(1)}, f32[96,8,4,128]{3,0,2,1:T(8,128)}) conditional(s32[]{:T(128)} %bitcast.8, () %tuple.21, (s32[96]{0:T(128)S(1)}, s32[6144]{0:T(1024)S(1)}, pred[8,4]{1,0:T(8,128)(4,1)S(1)}, s32[6144]{0:T(1024)S(1)}, s32[32]{0:T(128)S(1)}, /*index=5*/s32[32]{0:T(128)S(1)}, bf16[192,4096]{1,0:T(8,128)(2,1)S(1)}, ...), branch_computations={%region_0.0_spmd, %region_1.4_spmd} | conditional | flops 10081072128 | bytes 269895488 | solution.py:69
  385.3 0.3 compare_or_fusion
  385.7 0.4 broadcast_compare_fusion
  386.2 1.4 reshape.145
  387.6 0.3 broadcast_subtract_fusion
  387.9 36.9 %fusion = (f32[96,8,4]{0,2,1:T(4,128)S(1)}, f32[8,6144,96,4]{1,2,3,0:T(8,128)}) fusion(s32[8,4]{1,0:T(8,128)S(1)} %lt.62, s32[96,6144]{1,0:T(8,128)S(1)} %broadcast_subtract_fusion, pred[8,4,6144]{2,1,0:T(4,128)(4,1)S(1)} %compare_or_fusion, pred[96,6144]{1,0:T(8,128)(4,1)S(1)} %broadcast_compare_fusion, bf16[96,8,4,128]{3,2,1,0:T(4,128)(2,1)} %reshape.145, ...), kind=kOutput, calls=%fused_computation.3 | convolution fusion | flops 4945081344 | bytes 92024960 | tf_op jit(solution)/shard_map/cond/branch_1_fun/qgjd,kgd->qgjk/dot_general | solution.py:39
  424.8 35.3 %fusion.10 = f32[96,8,4,128]{3,0,2,1:T(8,128)} fusion(bf16[6144,8,128]{0,2,1:T(8,128)(2,1)} %get-tuple-element.95, f32[8,6144,96,4]{1,2,3,0:T(8,128)} %get-tuple-element.106, f32[96,8,4]{0,2,1:T(4,128)S(1)} %broadcast_maximum_fusion, s32[8,4]{1,0:T(8,128)S(1)} %lt.62, s32[96,6144]{1,0:T(8,128)S(1)} %broadcast_subtract_fusion, ...), kind=kOutput, calls=%fused_computation.12 | convolution fusion | flops 4982833152 | bytes 92811392 | tf_op jit(solution)/shard_map/cond/branch_1_fun/qgjk,kgd->qgjd/dot_general | solution.py:52
  460.1 38.6 %fusion.2 = f32[96,8,4]{0,2,1:T(4,128)S(1)} fusion(f32[8,6144,96,4]{1,2,3,0:T(8,128)} %get-tuple-element.106, f32[96,8,4]{0,2,1:T(4,128)S(1)} %broadcast_maximum_fusion, s32[8,4]{1,0:T(8,128)S(1)} %lt.62, s32[96,6144]{1,0:T(8,128)S(1)} %broadcast_subtract_fusion, pred[8,4,6144]{2,1,0:T(4,128)(4,1)S(1)} %compare_or_fusion, ...), kind=kLoop, calls=%fused_computation.5 | loop fusion | flops 150991872 | bytes 78667904 | tf_op jit(solution)/shard_map/cond/branch_1_fun/reduce_sum | solution.py:51
  499.2 1.9 divide_convert_fusion.1
  501.1 0.4 copy.25
  501.5 1.5 convert_element_type.36
  503.0 116.2 %conditional.3 = (f32[96,8,4]{0,2,1:T(4,128)S(1)}, f32[96,8,4,128]{3,0,2,1:T(8,128)}) conditional(s32[]{:T(128)} %bitcast.12, () %tuple.23, (s32[96]{0:T(128)S(1)}, s32[6144]{0:T(1024)S(1)}, pred[8,4]{1,0:T(8,128)(4,1)S(1)}, s32[6144]{0:T(1024)S(1)}, s32[32]{0:T(128)S(1)}, /*index=5*/s32[32]{0:T(128)S(1)}, bf16[192,4096]{1,0:T(8,128)(2,1)}, ...), branch_computations={%region_4.5_spmd, %region_5.8_spmd} | conditional | flops 10081072128 | bytes 269895488 | solution.py:69
  503.1 0.3 compare_or_fusion.1
  503.5 0.4 broadcast_compare_fusion.1
  503.9 1.2 slice.15
  505.1 1.4 reshape.146
  506.6 0.3 broadcast_subtract_fusion.1
  506.8 38.2 %fusion.19 = (f32[96,8,4]{0,2,1:T(4,128)S(1)}, f32[8,6144,96,4]{1,2,3,0:T(8,128)}) fusion(s32[8,4]{1,0:T(8,128)S(1)} %lt.70, s32[96,6144]{1,0:T(8,128)S(1)} %broadcast_subtract_fusion.1, pred[8,4,6144]{2,1,0:T(4,128)(4,1)S(1)} %compare_or_fusion.1, pred[96,6144]{1,0:T(8,128)(4,1)S(1)} %broadcast_compare_fusion.1, bf16[96,8,4,128]{3,2,1,0:T(4,128)(2,1)} %reshape.146, ...), kind=kOutput, calls=%fused_computation.24 | convolution fusion | flops 4945081344 | bytes 92024960 | tf_op jit(solution)/shard_map/cond/branch_1_fun/qgjd,kgd->qgjk/dot_general | solution.py:39
  545.1 35.3 %fusion.29 = f32[96,8,4,128]{3,0,2,1:T(8,128)} fusion(bf16[6144,8,128]{0,2,1:T(8,128)(2,1)} %get-tuple-element.104, f32[8,6144,96,4]{1,2,3,0:T(8,128)} %get-tuple-element.108, f32[96,8,4]{0,2,1:T(4,128)S(1)} %broadcast_maximum_fusion.1, s32[8,4]{1,0:T(8,128)S(1)} %lt.70, s32[96,6144]{1,0:T(8,128)S(1)} %broadcast_subtract_fusion.1, ...), kind=kOutput, calls=%fused_computation.33 | convolution fusion | flops 4982833152 | bytes 92811392 | tf_op jit(solution)/shard_map/cond/branch_1_fun/qgjk,kgd->qgjd/dot_general | solution.py:52
  580.3 38.6 %fusion.21 = f32[96,8,4]{0,2,1:T(4,128)S(1)} fusion(f32[8,6144,96,4]{1,2,3,0:T(8,128)} %get-tuple-element.108, f32[96,8,4]{0,2,1:T(4,128)S(1)} %broadcast_maximum_fusion.1, s32[8,4]{1,0:T(8,128)S(1)} %lt.70, s32[96,6144]{1,0:T(8,128)S(1)} %broadcast_subtract_fusion.1, pred[8,4,6144]{2,1,0:T(4,128)(4,1)S(1)} %compare_or_fusion.1, ...), kind=kLoop, calls=%fused_computation.26 | loop fusion | flops 150991872 | bytes 78667904 | tf_op jit(solution)/shard_map/cond/branch_1_fun/reduce_sum | solution.py:51
  619.1 1.9 divide_convert_fusion
  621.0 0.4 copy.28
  621.5 0.6 convert_element_type.40
  622.1 15.4 %convolution_convert_fusion = bf16[192,4096]{1,0:T(8,128)(2,1)} fusion(bf16[4096,4096]{1,0:T(8,128)(2,1)} %param.15, bf16[96,4096]{1,0:T(8,128)(2,1)S(1)} %convert_element_type.40, bf16[96,4096]{1,0:T(8,128)(2,1)} %convert_element_type.36), kind=kOutput, calls=%fused_computation.42 | convolution fusion | flops 6446383104 | bytes 36700160 | tf_op jit(solution)/shard_map/dot_general | solution.py:101
  (22 shorter events, 0.5 us)
Async XLA Ops:
  6.5 17.9 %copy-start.2 = (s32[32]{0:T(128)S(1)}, s32[32]{0:T(128)}, u32[]{:S(2)}) copy-start(s32[32]{0:T(128)} %param.13) | copy-start | bytes 388
  6.5 18.0 %copy-start.1 = (s32[2,32]{1,0:T(2,128)S(1)}, s32[2,32]{1,0:T(2,128)}, u32[]{:S(2)}) copy-start(s32[2,32]{1,0:T(2,128)} %param.14) | copy-start | bytes 772
  13.8 342.7 %all-to-all-start = ((bf16[32,192,1024]{2,1,0:T(8,128)(2,1)}), bf16[32,192,1024]{2,1,0:T(8,128)(2,1)}, u32[]{:S(2)}, u32[]{:S(2)}) async-start(bf16[32,192,1024]{2,1,0:T(8,128)(2,1)} %stack.2), calls=%async_computation | async-start | bytes 25165824 | tf_op jit(solution)/shard_map/all_to_all | solution.py:77
  21.2 347.1 %all-gather.2.cloned.1.call-start = ((), (), s32[]{:S(2)}) async-start(), calls=%async_computation.1 | async-start | bytes 12976128 | tf_op jit(solution)/shard_map/all_gather | solution.py:80
  368.3 16.8 %copy-start = (bf16[192,4096]{1,0:T(8,128)(2,1)S(1)}, bf16[192,4096]{1,0:T(8,128)(2,1)}, u32[]{:S(2)}) copy-start(bf16[192,4096]{1,0:T(8,128)(2,1)} %param.10) | copy-start | bytes 4718596
Sparse Core Ops, SparseCore 0:
  24.9 217.5 all-gather.1
